TPU v7x, 32 devices: a whole 2x2x4 slice. The times are simulated.
32 devices in a mesh: groups: 2 (over x), ctx: 16 (over z, y, core).
Axes of the slice: x: 2, y: 2, z: 4, core: 2. Of those that a mesh axis runs over, the one named last changes fastest.
Arguments:
- queries: bfloat16 [512, 128, 576], P(('groups', 'ctx')), parts along dimension 0, may hold values from -4 to 4
- latent_cache: bfloat16 [32768, 576], P(('groups', 'ctx')), parts along dimension 0, may hold values from -4 to 4
- block_picks: int32 [32, 32], P(('groups', 'ctx')), parts along dimension 0, may hold values from 0 to 255, as said below
- lengths: int32 [512], P(('groups', 'ctx')), parts along dimension 0, may hold values from 8192 to 16384
Outputs:
- latent_out: bfloat16 [512, 128, 512], P(('groups', 'ctx')), parts along dimension 0
There are 2 independent parts, one for each index of `groups`. A program takes and returns all parts, laid end to end along the dimension named above; each array names one. Nothing has to cross between parts.
Inputs may be any that keep to these rules, and one draw needn't show every extreme that they name: `block_picks`: each row names 32 different blocks. At most 4 of a row's blocks lie in one owner's range of 16 consecutive blocks, and every row reaches this with its first 4 entries, which lie in the first half of the context. Over all rows together at most 8 different blocks of one owner's range are named, and some owner reaches this.
All inputs are finite; a program needn't handle non-finite values.
Results may differ from a plain program's by a relative error of at most 0.0035.
Values may be sent and summed in bfloat16 or wider, within the bound.
A program may use at most 128 MiB of HBM per device.

v0:
```python
import jax
import jax.numpy as jnp
from jax import lax
from jax.sharding import PartitionSpec as P

LAT = 512
BLOCK = 64
TOPK = 32


SOFTMAX_SCALE = 192.0 ** (-0.5)


def attend(query_rows, key_rows, positions, row_lengths):
    total_rows = query_rows.shape[0]
    step_rows = 512
    block_count = total_rows // step_rows
    latent = key_rows[:, :LAT]

    def per_block(inputs):
        block_queries, block_lengths = inputs
        block_ratings = (
            lax.dot_general(
                block_queries,
                key_rows,
                (((1,), (1,)), ((), ())),
                preferred_element_type=jnp.float32,
            )
            * SOFTMAX_SCALE
        )
        visible = positions[None, :] < block_lengths[:, None]
        row_max = jnp.max(jnp.where(visible, block_ratings, -jnp.inf), axis=1, keepdims=True)
        exponent = jnp.where(visible, jnp.exp(block_ratings - row_max), 0.0)
        normaliser = jnp.sum(exponent, axis=1, keepdims=True)
        weights = exponent.astype(jnp.bfloat16)
        result = jnp.dot(weights, latent, preferred_element_type=jnp.float32) / normaliser
        return result.astype(jnp.bfloat16)

    outputs = lax.map(
        per_block,
        (
            query_rows.reshape(block_count, step_rows, query_rows.shape[1]),
            row_lengths.reshape(block_count, step_rows),
        ),
    )
    return outputs.reshape(total_rows, LAT)


def shards(queries, latent_cache, block_picks, lengths):
    ctx_count = lax.axis_size("ctx")
    myself = lax.axis_index("ctx")
    feature = latent_cache.shape[1]
    owned = latent_cache.shape[0] // BLOCK
    capacity = max(1, 2 * TOPK // ctx_count)
    block_rows = latent_cache.reshape(owned, BLOCK * feature)
    own_picks = block_picks[0]
    owners = own_picks // owned
    union_size = 2 * capacity
    all_picks = lax.all_gather(block_picks, "ctx", axis=0, tiled=True)
    selected_flag = (
        jnp.zeros((ctx_count * owned,), jnp.int32)
        .at[all_picks.reshape(-1)]
        .set(1)
        .reshape(ctx_count, owned)
    )
    packed_at = jnp.cumsum(selected_flag, axis=1) - 1
    own_flag = lax.dynamic_index_in_dim(selected_flag, myself, 0, keepdims=False)
    own_packed = lax.dynamic_index_in_dim(packed_at, myself, 0, keepdims=False)
    slot_ids = jnp.arange(union_size, dtype=jnp.int32)
    matches = (own_packed[None, :] == slot_ids[:, None]) & (own_flag[None, :] == 1)
    source = jnp.sum(
        matches.astype(jnp.int32) * jnp.arange(owned, dtype=jnp.int32)[None, :], axis=1
    )
    candidates = jnp.take(block_rows, source, axis=0)
    target = owners * union_size + jnp.take(packed_at.reshape(-1), own_picks)
    portion = lax.all_gather(candidates, "ctx", axis=0, tiled=True)
    indices = jnp.arange(portion.shape[0], dtype=jnp.int32)
    pick_one = (target[:, None] == indices[None, :]).astype(jnp.bfloat16)
    chosen = jnp.dot(pick_one, portion, preferred_element_type=jnp.float32).astype(jnp.bfloat16)
    key_rows = chosen.reshape(TOPK * BLOCK, feature)
    within = jnp.arange(BLOCK, dtype=jnp.int32)
    positions = (own_picks[:, None] * BLOCK + within[None, :]).reshape(-1)
    head_count = queries.shape[1]
    query_rows = queries.reshape(queries.shape[0] * head_count, feature)
    row_lengths = jnp.repeat(lengths, head_count)
    result = attend(query_rows, key_rows, positions, row_lengths)
    return result.reshape(queries.shape[0], head_count, LAT)


def solution(mesh):
    placed = (
        P(("groups", "ctx"), None, None),
        P(("groups", "ctx"), None),
        P(("groups", "ctx"), None),
        P(("groups", "ctx")),
    )
    return jax.shard_map(
        shards,
        mesh=mesh,
        in_specs=placed,
        out_specs=P(("groups", "ctx"), None, None),
        check_vma=False,
    )
```

profile of v0, /device:TPU:0, one launch (start us, length us, event | category | flops | bytes accessed | tf_op | source)
XLA Modules:
  0.0 166.6 jit_solution(2164973816998494499)
XLA Ops:
  6.5 0.0 all-gather.3.cloned.1.call-start
  6.5 23.3 %all-gather = s32[16,1,32]{2,1,0:T(1,128)S(1)} all-gather(s32[1,1,32]{2,1,0:T(1,128)} %bitcast.62), channel_id=1, replica_groups=mesh['groups'=2,'ctx'=16] {'ctx'}, dimensions={0}, use_global_device_ids=true | all-gather | bytes 2176 | tf_op jit(solution)/shard_map/all_gather | solution.py:59
  29.8 0.5 broadcast.185
  30.3 0.7 reduce.3
  31.0 0.1 reshape.149
  31.1 2.4 %scatter_custom_fusion = s32[256]{0:T(256)S(1)} fusion(s32[512]{0:T(512)S(1)} %bitcast.61, s32[512]{0:T(512)S(1)} %broadcast.154, s32[]{:T(128)} %copy.24), kind=kCustom, calls=%fused_computation.56 | custom fusion | bytes 1028 | tf_op jit(solution)/shard_map/scatter | solution.py:63
  33.5 0.1 reshape.150
  33.6 0.2 reduce_window_sum.11
  33.8 0.1 select_reduce_fusion
  34.0 1.7 %copy.12 = bf16[1024,576]{1,0:T(8,128)(2,1)S(1)} copy(bf16[1024,576]{0,1:T(8,128)(2,1)} %param.7) | data formatting | bytes 2359296 | tf_op args[1]
  35.7 1.6 reshape.151
  37.3 0.0 copy-start
  37.3 1.7 %gather_fusion.1 = bf16[8,36864]{1,0:T(8,128)(2,1)} fusion(bf16[16,36864]{1,0:T(8,128)(2,1)S(1)} %reshape.151, s32[1024]{0:T(1024)S(1)} %pad_clamp_fusion), kind=kCustom, calls=%fused_computation.1 | custom fusion | bytes 1179680 | tf_op jit(solution)/shard_map/jit(_take)/gather | solution.py:74
  39.1 0.0 copy-start.2
  39.1 0.0 copy-start.1
  39.1 2.0 %broadcast_select_fusion = bf16[8,36864]{1,0:T(8,128)(2,1)} fusion(bf16[8,36864]{1,0:T(8,128)(2,1)} %gather_fusion.1, pred[8]{0:T(512)(128)(4,1)S(1)} %compare_and_fusion), kind=kLoop, calls=%fused_computation.27 | loop fusion | flops 294912 | bytes 1179656 | tf_op jit(solution)/shard_map/jit(_take)/select_n | solution.py:74
  41.1 0.0 all-gather.3.cloned.1.call-update
  41.1 0.1 sub.22
  41.2 0.0 copy-done
  41.2 2.6 %copy.11 = bf16[16,128,576]{2,1,0:T(8,128)(2,1)} copy(bf16[16,128,576]{1,2,0:T(8,128)(2,1)S(1)} %copy-done) | data formatting | bytes 4718592 | tf_op args[0]
  43.7 0.0 copy-done.2
  43.8 0.1 broadcast_in_dim.55
  43.8 0.1 broadcast_bitcast_fusion
  43.9 0.0 copy-done.1
  43.9 0.7 gather_fusion
  44.7 74.8 %all-gather.3.cloned.1.call-done = bf16[128,36864]{1,0:T(8,128)(2,1)} async-done(((bf16[8,36864]{1,0:T(8,128)(2,1)}), bf16[128,36864]{1,0:T(8,128)(2,1)}) %all-gather.3.cloned.1.call-update) | async-done | bytes 9437200 | tf_op jit(solution)/shard_map/all_gather | solution.py:76
  119.4 5.1 %convolution_convert_fusion = bf16[32,36864]{1,0:T(8,128)(2,1)S(1)} fusion(bf16[128,36864]{1,0:T(8,128)(2,1)} %all-gather.3.cloned.1.call-done, s32[32]{0:T(128)S(1)} %get-tuple-element.77), kind=kOutput, calls=%fused_computation.26 | convolution fusion | flops 303173632 | bytes 11796608 | tf_op jit(solution)/shard_map/dot_general | solution.py:79
  124.5 4.1 %reshape.152 = bf16[2048,576]{1,0:T(8,128)(2,1)} reshape(bf16[32,36864]{1,0:T(8,128)(2,1)S(1)} %convolution_convert_fusion) | data formatting | bytes 4718592 | tf_op jit(solution)/shard_map/reshape | solution.py:80
  128.6 0.0 slice-start
  128.6 1.6 slice-done
  130.2 29.5 %while.11 = (s32[]{:T(128)}, bf16[4,512,512]{2,1,0:T(8,128)(2,1)}, s32[4,512]{1,0:T(4,128)S(1)}, bf16[4,512,576]{2,1,0:T(8,128)(2,1)}, bf16[2048,576]{1,0:T(8,12...) while((s32[]{:T(128)}, bf16[4,512,512]{2,1,0:T(8,128)(2,1)}, ...), condition=%wide.region_6.7_spmd.clone, body=%wide.region_3.6_spmd.clone.sunk | while | flops 2296906752 | bytes 18552024 | solution.py:39
  130.2 0.1 iota_add_fusion.2
  130.3 0.1 lt.139
  130.4 3.9 %fusion.45 = (f32[512]{0:T(512)S(1)}, f32[512,2048]{1,0:T(8,128)S(1)}) fusion(s32[2048]{0:T(1024)S(1)} %lt.139, s32[512]{0:T(512)S(1)} %bitcast.57, bf16[2048,576]{1,0:T(8,128)(2,1)} %get-tuple-element.145, bf16[4,512,576]{2,1,0:T(8,128)(2,1)} %get-tuple-element.144, s32[]{:T(128)} %get-tuple-element.133), kind=kOutput, calls=%fused_computation.6.clone.1 | convolution fusion | flops 1212153344 | bytes 7483904 | tf_op jit(solution)/shard_map/while/body/eval_jaxpr/dot_general | solution.py:23
  134.3 1.1 fusion.46
  135.4 2.2 %fusion.47 = bf16[4,512,512]{2,1,0:T(8,128)(2,1)} fusion(bf16[4,512,512]{2,1,0:T(8,128)(2,1)} %get-tuple-element.134, s32[]{:T(128)} %get-tuple-element.133, bf16[2048,512]{1,0:T(8,128)(2,1)S(1)} %get-tuple-element.146, f32[512,2048]{1,0:T(8,128)S(1)} %get-tuple-element.123, f32[512]{0:T(512)S(1)} %get-tuple-element.124, s32[2048]{0:T(1024)S(1)} %lt.139, ...), kind=kOutput, calls=%fused_computation.17.clone.1 | convolution fusion | flops 1079508992 | bytes 6830592 | tf_op jit(solution)/shard_map/while/body/eval_jaxpr/dot_general | solution.py:36
  137.6 0.1 iota_add_fusion.2
  137.7 0.1 lt.139
  137.8 3.9 %fusion.45 = (f32[512]{0:T(512)S(1)}, f32[512,2048]{1,0:T(8,128)S(1)}) fusion(s32[2048]{0:T(1024)S(1)} %lt.139, s32[512]{0:T(512)S(1)} %bitcast.57, bf16[2048,576]{1,0:T(8,128)(2,1)} %get-tuple-element.145, bf16[4,512,576]{2,1,0:T(8,128)(2,1)} %get-tuple-element.144, s32[]{:T(128)} %get-tuple-element.133), kind=kOutput, calls=%fused_computation.6.clone.1 | convolution fusion | flops 1212153344 | bytes 7483904 | tf_op jit(solution)/shard_map/while/body/eval_jaxpr/dot_general | solution.py:23
  141.7 1.1 fusion.46
  142.8 2.2 %fusion.47 = bf16[4,512,512]{2,1,0:T(8,128)(2,1)} fusion(bf16[4,512,512]{2,1,0:T(8,128)(2,1)} %get-tuple-element.134, s32[]{:T(128)} %get-tuple-element.133, bf16[2048,512]{1,0:T(8,128)(2,1)S(1)} %get-tuple-element.146, f32[512,2048]{1,0:T(8,128)S(1)} %get-tuple-element.123, f32[512]{0:T(512)S(1)} %get-tuple-element.124, s32[2048]{0:T(1024)S(1)} %lt.139, ...), kind=kOutput, calls=%fused_computation.17.clone.1 | convolution fusion | flops 1079508992 | bytes 6830592 | tf_op jit(solution)/shard_map/while/body/eval_jaxpr/dot_general | solution.py:36
  145.0 0.1 iota_add_fusion.2
  145.1 0.1 lt.139
  145.1 3.9 %fusion.45 = (f32[512]{0:T(512)S(1)}, f32[512,2048]{1,0:T(8,128)S(1)}) fusion(s32[2048]{0:T(1024)S(1)} %lt.139, s32[512]{0:T(512)S(1)} %bitcast.57, bf16[2048,576]{1,0:T(8,128)(2,1)} %get-tuple-element.145, bf16[4,512,576]{2,1,0:T(8,128)(2,1)} %get-tuple-element.144, s32[]{:T(128)} %get-tuple-element.133), kind=kOutput, calls=%fused_computation.6.clone.1 | convolution fusion | flops 1212153344 | bytes 7483904 | tf_op jit(solution)/shard_map/while/body/eval_jaxpr/dot_general | solution.py:23
  149.1 1.1 fusion.46
  150.2 2.2 %fusion.47 = bf16[4,512,512]{2,1,0:T(8,128)(2,1)} fusion(bf16[4,512,512]{2,1,0:T(8,128)(2,1)} %get-tuple-element.134, s32[]{:T(128)} %get-tuple-element.133, bf16[2048,512]{1,0:T(8,128)(2,1)S(1)} %get-tuple-element.146, f32[512,2048]{1,0:T(8,128)S(1)} %get-tuple-element.123, f32[512]{0:T(512)S(1)} %get-tuple-element.124, s32[2048]{0:T(1024)S(1)} %lt.139, ...), kind=kOutput, calls=%fused_computation.17.clone.1 | convolution fusion | flops 1079508992 | bytes 6830592 | tf_op jit(solution)/shard_map/while/body/eval_jaxpr/dot_general | solution.py:36
  152.4 0.1 iota_add_fusion.2
  152.4 0.1 lt.139
  152.5 3.9 %fusion.45 = (f32[512]{0:T(512)S(1)}, f32[512,2048]{1,0:T(8,128)S(1)}) fusion(s32[2048]{0:T(1024)S(1)} %lt.139, s32[512]{0:T(512)S(1)} %bitcast.57, bf16[2048,576]{1,0:T(8,128)(2,1)} %get-tuple-element.145, bf16[4,512,576]{2,1,0:T(8,128)(2,1)} %get-tuple-element.144, s32[]{:T(128)} %get-tuple-element.133), kind=kOutput, calls=%fused_computation.6.clone.1 | convolution fusion | flops 1212153344 | bytes 7483904 | tf_op jit(solution)/shard_map/while/body/eval_jaxpr/dot_general | solution.py:23
  156.4 1.1 fusion.46
  157.6 2.2 %fusion.47 = bf16[4,512,512]{2,1,0:T(8,128)(2,1)} fusion(bf16[4,512,512]{2,1,0:T(8,128)(2,1)} %get-tuple-element.134, s32[]{:T(128)} %get-tuple-element.133, bf16[2048,512]{1,0:T(8,128)(2,1)S(1)} %get-tuple-element.146, f32[512,2048]{1,0:T(8,128)S(1)} %get-tuple-element.123, f32[512]{0:T(512)S(1)} %get-tuple-element.124, s32[2048]{0:T(1024)S(1)} %lt.139, ...), kind=kOutput, calls=%fused_computation.17.clone.1 | convolution fusion | flops 1079508992 | bytes 6830592 | tf_op jit(solution)/shard_map/while/body/eval_jaxpr/dot_general | solution.py:36
  (17 shorter events, 0.1 us)
Async XLA Ops:
  6.5 112.9 %all-gather.3.cloned.1.call-start = ((), (), s32[]{:S(2)}) async-start(), calls=%async_computation | async-start | bytes 10027008 | tf_op jit(solution)/shard_map/all_gather | solution.py:76
  37.3 3.9 %copy-start = (bf16[16,128,576]{1,2,0:T(8,128)(2,1)S(1)}, bf16[16,128,576]{1,2,0:T(8,128)(2,1)}, u32[]{:S(2)}) copy-start(bf16[16,128,576]{1,2,0:T(8,128)(2,1)} %param.6) | copy-start | bytes 7077892
  39.1 4.7 %copy-start.2 = (s32[16]{0:T(128)S(1)}, s32[16]{0:T(128)}, u32[]{:S(2)}) copy-start(s32[16]{0:T(128)} %param.9) | copy-start | bytes 196
  39.1 4.9 %copy-start.1 = (s32[1,32]{1,0:T(1,128)S(1)}, s32[1,32]{1,0:T(1,128)}, u32[]{:S(2)}) copy-start(s32[1,32]{1,0:T(1,128)} %param.8) | copy-start | bytes 388
  128.6 1.6 slice-start
Sparse Core Ops, SparseCore 0:
  41.2 78.1 all-gather.2
where the time goes:
time: 167 us
  waiting for transfers between devices  74.8 us (45%)
  matrix products  29.5 us (18%)
  blocking collectives  23.3 us (14%)
  local copies, waits for them, and re-layouts  17.7 us (11%)
  between operations  13.5 us (8%)
  other arithmetic  7.79 us (5%)
    all_gather x1, waiting for transfers between devices, shards(): portion = lax.all_gather(candidates, 'ctx', axis=0, tiled=True)  74.8 us
    all_gather x1, blocking collectives, shards(): all_picks = lax.all_gather(block_picks, 'ctx', axis=0, tiled=True)  23.3 us
    dot_general x4, matrix products, per_block(): lax.dot_general(block_queries, key_rows, (((1,), (1,)), ((), ())), prefer...  15.7 us
    dot_general x4, matrix products, per_block(): jnp.dot(weights, latent, preferred_element_type=jnp.float32) / normaliser  8.69 us
    dot_general x1, matrix products, shards(): jnp.dot(pick_one, portion, preferred_element_type=jnp.float32)  5.07 us
    reduce_sum x4, other arithmetic, per_block(): normaliser = jnp.sum(exponent, axis=1, keepdims=True)  4.46 us
    unnamed x10, local copies, waits for them, and re-layouts  4.33 us
    reshape x1, local copies, waits for them, and re-layouts, shards(): key_rows = chosen.reshape(TOPK * BLOCK, feature)  4.14 us
  transfers between devices with their start and end apart: 1, of which 1 were waited for; matrix products, arithmetic and copies ran while one was open for 2% of the time, Pallas kernels for 0%

commit v1 on v0

v1 whole, which is shorter than its diff:
```python
import functools

import jax
import jax.numpy as jnp
from jax import lax
from jax.experimental import pallas as pl
from jax.experimental.pallas import tpu as pltpu
from jax.sharding import PartitionSpec as P

LAT = 512
BLOCK = 64
TOPK = 32
LANES = 128

SOFTMAX_SCALE = 192.0 ** (-0.5)
LOG2E = 1.4426950408889634
MESH = pl.DeviceIdType.MESH
HIDDEN = -1e30


def gather_kernel(
    ctx_count, owned, units, picks_ref, flags_ref, cache_ref, keys_ref,
    all_flags, gath, flag_send, flag_recv, send, recv,
):
    feature = cache_ref.shape[2]
    rope = feature - LAT
    pair = 2 * BLOCK
    tall = pair * rope // LAT
    line = ctx_count // 4
    me = lax.axis_index("ctx")
    core = lax.rem(me, 2)
    y = lax.rem(me // 2, 2)
    z = me // 4

    def at(zz, yy, cc):
        return (zz * 2 + yy) * 2 + cc

    barrier = pltpu.get_barrier_semaphore()

    @pl.loop(1, ctx_count)
    def _(d):
        pl.semaphore_signal(
            barrier, inc=1, device_id={"ctx": lax.rem(me + d, ctx_count)}, device_id_type=MESH
        )

    pl.semaphore_wait(barrier, ctx_count - 1)

    def flag_copy(d):
        return pltpu.make_async_remote_copy(
            src_ref=flags_ref,
            dst_ref=all_flags.at[me],
            send_sem=flag_send.at[d],
            recv_sem=flag_recv.at[me],
            device_id={"ctx": lax.rem(me + d, ctx_count)},
            device_id_type=MESH,
        )

    def flag_arrival(source):
        return pltpu.make_async_remote_copy(
            src_ref=flags_ref,
            dst_ref=all_flags.at[source],
            send_sem=flag_send.at[0],
            recv_sem=flag_recv.at[source],
            device_id={"ctx": source},
            device_id_type=MESH,
        )

    @pl.loop(1, ctx_count)
    def _(d):
        flag_copy(d).start()

    all_flags[me] = flags_ref[...]

    @pl.loop(1, ctx_count)
    def _(d):
        flag_arrival(lax.rem(me + d, ctx_count)).wait_recv()

    named = jnp.minimum(jnp.max(all_flags[...], axis=0), 1)
    rows = named.shape[0]
    block_id = lax.broadcasted_iota(jnp.int32, (rows, LANES), 0) * LANES + lax.broadcasted_iota(
        jnp.int32, (rows, LANES), 1
    )
    mine = (named > 0) & (block_id // owned == me)

    def unit_copy(slot, local, way, target):
        return pltpu.make_async_remote_copy(
            src_ref=gath.at[slot],
            dst_ref=gath.at[slot],
            send_sem=send.at[local, way],
            recv_sem=recv.at[slot],
            device_id={"ctx": target},
            device_id_type=MESH,
        )

    def slot_of(zz, j):
        crossed = (j == units).astype(jnp.int32)
        yy = lax.rem(y + crossed, 2)
        u = j * (1 - crossed)
        return at(zz, yy, core) * units + u, (zz * 2 + yy) * units + u

    up = at(lax.rem(z + 1, line), y, core)
    down = at(lax.rem(z + line - 1, line), y, core)
    across = at(z, 1 - y, core)
    sibling = at(z, y, 1 - core)

    def sends(zz, j):
        valid = (zz >= 0) & (zz < line) & ((j < units) | (core == 1))
        own_line = j < units
        return (
            (0, up, valid & (zz <= z) & (z + 1 < line)),
            (1, down, valid & (zz >= z) & (z > 0)),
            (2, across, valid & own_line & ((zz == z) | (core == 0) | (j > 0))),
            (3, sibling, valid),
        )

    def forward(zz, j, skip=()):
        slot, local = slot_of(zz, j)
        for way, target, yes in sends(zz, j):
            if way not in skip:
                @pl.when(yes)
                def _():
                    unit_copy(slot, local, way, target).start()

    def arrived(slot):
        unit_copy(slot, 0, 0, sibling).wait_recv()

    past = ctx_count * owned
    last = jnp.int32(-1)
    for u in range(units):
        for h in range(2):
            last = jnp.min(jnp.where(mine & (block_id > last), block_id, past))
            tokens = cache_ref[jnp.minimum(last - me * owned, owned - 1)]
            gath[me * units + u, h * BLOCK : (h + 1) * BLOCK, :] = tokens[:, :LAT]
            tail = tokens[:, LAT:]
            parts = [tail[i * tall : (i + 1) * tall, :] for i in range(BLOCK // tall)]
            gath[me * units + u, pair:, h * (LAT // 2) : (h + 1) * (LAT // 2)] = jnp.concatenate(
                parts, axis=1
            )
        forward(z, jnp.int32(u))

    per = units + 1

    @pl.loop(0, per * (line - 1))
    def _(k):
        step = k // per
        j = lax.rem(k, per)
        for zz in (z + 1 + step, z - 1 - step):
            @pl.when((zz >= 0) & (zz < line) & ((j < units) | (core == 1)))
            def _():
                slot, _ = slot_of(zz, j)
                arrived(slot)
                forward(zz, j)

        @pl.when((k == 0) & (core == 1))
        def _():
            slot, _ = slot_of(z, jnp.int32(units))
            arrived(slot)
            forward(z, jnp.int32(units))

    @pl.loop(0, units * line)
    def _(k):
        zz = lax.rem(z + k // units, line)
        j = lax.rem(k, units)

        @pl.when((core == 0) | (j > 0))
        def _():
            slot = at(zz, 1 - y, core) * units + j
            local = (zz * 2 + 1 - y) * units + j
            arrived(slot)
            unit_copy(slot, local, 3, sibling).start()

    @pl.loop(0, 2 * line)
    def _(o):
        @pl.loop(0, units)
        def _(u):
            arrived((o * 2 + 1 - core) * units + u)

    for k in range(TOPK):
        p = picks_ref[0, k]
        owner = p // owned
        slot = jnp.sum(jnp.where((block_id // owned == owner) & (block_id < p), named, 0))
        unit = gath[owner * units + slot // 2]
        first = lax.rem(slot, 2) == 0
        keys_ref[k * BLOCK : (k + 1) * BLOCK, :LAT] = jnp.where(
            first, unit[:BLOCK], unit[BLOCK:pair]
        )
        tail = jnp.where(first, unit[pair:, : LAT // 2], unit[pair:, LAT // 2 :])
        keys_ref[k * BLOCK : (k + 1) * BLOCK, LAT:] = jnp.concatenate(
            [tail[:, i * rope : (i + 1) * rope] for i in range(BLOCK // tall)], axis=0
        )

    @pl.loop(1, ctx_count)
    def _(d):
        flag_copy(d).wait_send()

    @pl.loop(0, per * line)
    def _(k):
        zz = k // per
        j = lax.rem(k, per)
        slot, local = slot_of(zz, j)
        for way, target, yes in sends(zz, j):
            @pl.when(yes)
            def _():
                unit_copy(slot, local, way, target).wait_send()

    @pl.loop(0, units * line)
    def _(k):
        zz = k // units
        j = lax.rem(k, units)

        @pl.when((core == 0) | (j > 0))
        def _():
            slot = at(zz, 1 - y, core) * units + j
            local = (zz * 2 + 1 - y) * units + j
            unit_copy(slot, local, 3, sibling).wait_send()


def attend_kernel(per_step, lengths_ref, positions_ref, q_ref, keys_ref, out_ref):
    heads = q_ref.shape[1]
    feature = q_ref.shape[2]
    step = pl.program_id(0)
    q = q_ref[...].reshape(per_step * heads, feature)
    s = lax.dot_general(
        q, keys_ref[...], (((1,), (1,)), ((), ())), preferred_element_type=jnp.float32
    )
    for r in range(per_step):
        visible = positions_ref[...] < lengths_ref[step * per_step + r]
        part = jnp.where(visible, s[r * heads : (r + 1) * heads, :], HIDDEN)
        top = jnp.max(part, axis=1, keepdims=True)
        e = jnp.exp2((part - top) * (SOFTMAX_SCALE * LOG2E))
        total = jnp.sum(e, axis=1, keepdims=True)
        o = jnp.dot(
            e.astype(jnp.bfloat16), keys_ref[:, :LAT], preferred_element_type=jnp.float32
        )
        out_ref[r] = (o / total).astype(jnp.bfloat16)


def shards(queries, latent_cache, block_picks, lengths):
    ctx_count = lax.axis_size("ctx")
    feature = latent_cache.shape[1]
    owned = latent_cache.shape[0] // BLOCK
    units = max(1, 2 * TOPK // ctx_count)
    own_picks = block_picks[0]
    total = ctx_count * owned
    flags = jnp.sum(
        (own_picks[:, None] == jnp.arange(total, dtype=jnp.int32)[None, :]).astype(jnp.int32),
        axis=0,
    ).reshape(total // LANES, LANES)
    flags = jnp.pad(flags, ((0, -flags.shape[0] % 8), (0, 0)))
    within = jnp.arange(BLOCK, dtype=jnp.int32)
    positions = (own_picks[:, None] * BLOCK + within[None, :]).reshape(1, -1)
    tall = 2 * BLOCK + 2 * BLOCK * (feature - LAT) // LAT
    keys = pl.pallas_call(
        functools.partial(gather_kernel, ctx_count, owned, units),
        out_shape=jax.ShapeDtypeStruct((TOPK * BLOCK, feature), jnp.bfloat16),
        in_specs=[
            pl.BlockSpec(memory_space=pltpu.SMEM),
            pl.BlockSpec(memory_space=pltpu.VMEM),
            pl.BlockSpec(memory_space=pltpu.VMEM),
        ],
        out_specs=pl.BlockSpec(memory_space=pltpu.VMEM),
        scratch_shapes=[
            pltpu.VMEM((ctx_count,) + flags.shape, jnp.int32),
            pltpu.VMEM((ctx_count * units, tall, LAT), jnp.bfloat16),
            pltpu.SemaphoreType.DMA((ctx_count,)),
            pltpu.SemaphoreType.DMA((ctx_count,)),
            pltpu.SemaphoreType.DMA((ctx_count // 2 * units, 4)),
            pltpu.SemaphoreType.DMA((ctx_count * units,)),
        ],
        compiler_params=pltpu.CompilerParams(
            collective_id=0, has_side_effects=True, vmem_limit_bytes=40 * 1024 * 1024
        ),
    )(block_picks, flags, latent_cache.reshape(owned, BLOCK, feature))
    rows, heads, _ = queries.shape
    per_step = 2 if rows % 2 == 0 else 1
    return pl.pallas_call(
        functools.partial(attend_kernel, per_step),
        grid=(rows // per_step,),
        out_shape=jax.ShapeDtypeStruct((rows, heads, LAT), jnp.bfloat16),
        in_specs=[
            pl.BlockSpec(memory_space=pltpu.SMEM),
            pl.BlockSpec(memory_space=pltpu.VMEM),
            pl.BlockSpec((per_step, heads, feature), lambda i: (i, 0, 0)),
            pl.BlockSpec((TOPK * BLOCK, feature), lambda i: (0, 0)),
        ],
        out_specs=pl.BlockSpec((per_step, heads, LAT), lambda i: (i, 0, 0)),
        compiler_params=pltpu.CompilerParams(vmem_limit_bytes=40 * 1024 * 1024),
    )(lengths, positions, queries, keys)


def solution(mesh):
    placed = (
        P(("groups", "ctx"), None, None),
        P(("groups", "ctx"), None),
        P(("groups", "ctx"), None),
        P(("groups", "ctx")),
    )
    return jax.shard_map(
        shards,
        mesh=mesh,
        in_specs=placed,
        out_specs=P(("groups", "ctx"), None, None),
        check_vma=False,
    )
```

time: 167 us -> 94.4 us (0.57)
  Pallas kernels: 0 us -> 82.6 us
  waiting for transfers between devices: 74.8 us -> 0 us
  matrix products: 29.5 us -> 0 us
  blocking collectives: 23.3 us -> 0 us
  between operations: 13.5 us -> 0.02 us
  local copies, waits for them, and re-layouts: 17.7 us -> 9.89 us
  other arithmetic: 7.79 us -> 1.54 us
    pallas_call x0 -> x2, Pallas kernels: none -> 82.6 us  [the longest x1 65.7 us: shards(): pl.pallas_call(functools.partial(gather_kernel, ctx_count, owned, units),...]
    all_gather x1 -> x0, waiting for transfers between devices: 74.8 us -> none  [shards(): portion = lax.all_gather(candidates, 'ctx', axis=0, tiled=True)]
    dot_general x9 -> x0, matrix products: 29.5 us -> none  [the longest x4 15.7 us: per_block(): lax.dot_general(block_queries, key_rows, (((1,), (1,)), ((), ())), prefer...]
    all_gather x1 -> x0, blocking collectives: 23.3 us -> none  [shards(): all_picks = lax.all_gather(block_picks, 'ctx', axis=0, tiled=True)]
    reshape x4 -> x0, local copies, waits for them, and re-layouts: 5.91 us -> none  [the longest x1 4.14 us: shards(): key_rows = chosen.reshape(TOPK * BLOCK, feature)]
    unnamed x10, local copies, waits for them, and re-layouts: 4.33 us -> 9.8 us
    reduce_sum x5 -> x1, other arithmetic: 4.58 us -> 0.74 us  [shards(): jnp.sum((own_picks[:, None] == jnp.arange(total, dtype=jnp.int32)[None, :...]
    gather x2 -> x0, local copies, waits for them, and re-layouts: 2.46 us -> none  [the longest x1 1.75 us: shards(): candidates = jnp.take(block_rows, source, axis=0)]
  transfers between devices with their start and end apart: 1 -> 0, of which waited for: 1 -> 0; matrix products, arithmetic and copies ran while one was open for 2% -> 0% of each run, Pallas kernels for 0% -> 0%
where the time goes in v1:
time: 94.4 us; the launch traced here: 94.1 us
  Pallas kernels  82.6 us (88%)
  local copies, waits for them, and re-layouts  9.89 us (10%)
  other arithmetic  1.54 us (2%)
    pallas_call x1, Pallas kernels, shards(): pl.pallas_call(functools.partial(gather_kernel, ctx_count, owned, units),...  65.7 us
    pallas_call x1, Pallas kernels, shards(): pl.pallas_call(functools.partial(attend_kernel, per_step), grid=(rows //...  17 us
    unnamed x10, local copies, waits for them, and re-layouts  9.8 us

profile of v1, /device:TPU:0, one launch (start us, length us, event | category | flops | bytes accessed | tf_op | source)
XLA Modules:
  0.0 94.1 jit_solution(8071923763584410976)
XLA Ops:
  0.0 0.0 copy-start.2
  0.0 0.7 broadcast_multiply_fusion
  0.7 0.7 convert_reduce_fusion
  1.5 0.1 iota_add_fusion
  1.6 0.1 add.28.positions_ref
  1.6 2.4 %copy.7 = bf16[1024,576]{1,0:T(8,128)(2,1)} copy(bf16[1024,576]{0,1:T(8,128)(2,1)} %param.5) | data formatting | bytes 2359296 | tf_op args[1]
  4.0 0.0 copy-done.2
  4.0 0.0 copy-start.1
  4.0 1.3 %copy-done.1 = bf16[1024,576]{1,0:T(8,128)(2,1)S(1)} copy-done((bf16[1024,576]{1,0:T(8,128)(2,1)S(1)}, bf16[1024,576]{1,0:T(8,128)(2,1)}, u32[]{:S(2)}) %copy-start.1) | copy-done | bytes 1179672
  5.4 65.7 %shard_map.46.keys_ref = bf16[2048,576]{1,0:T(8,128)(2,1)S(1)} custom-call(s32[1,32]{1,0:T(1,128)S(1)} %copy-done.2, s32[8,128]{1,0:T(8,128)S(1)} %pad.4.flags_ref, bf16[16,64,576]{2,1,0:T(8,128)(2,1)S(1)} %bitcast.4), custom_call_target="tpu_custom_call" | custom-call | tf_op jit(solution)/shard_map/pallas_call | solution.py:253
  71.0 0.0 copy-start.3
  71.1 4.3 %copy.8.q_ref = bf16[16,128,576]{2,1,0:T(8,128)(2,1)} copy(bf16[16,128,576]{1,2,0:T(8,128)(2,1)} %param.4) | data formatting | bytes 4718592 | tf_op args[0]
  75.4 0.0 copy-done.3
  75.4 0.0 copy-start
  75.4 1.7 %copy-done = bf16[16,128,576]{2,1,0:T(8,128)(2,1)S(1)} copy-done((bf16[16,128,576]{2,1,0:T(8,128)(2,1)S(1)}, bf16[16,128,576]{2,1,0:T(8,128)(2,1)}, u32[]{:S(2)}) %copy-start) | copy-done | bytes 2359320
  77.1 17.0 %shard_map.47 = bf16[16,128,512]{2,1,0:T(8,128)(2,1)} custom-call(s32[16]{0:T(128)S(1)} %copy-done.3, s32[1,2048]{1,0:T(1,128)S(1)} %add.28.positions_ref, bf16[16,128,576]{2,1,0:T(8,128)(2,1)S(1)} %copy-done, bf16[2048,576]{1,0:T(8,128)(2,1)S(1)} %shard_map.46.keys_ref), custom_call_target="tpu_custom_call" | custom-call | tf_op jit(solution)/shard_map/pallas_call | solution.py:276
  (1 shorter events, 0.0 us)
Async XLA Ops:
  0.0 4.0 %copy-start.2 = (s32[1,32]{1,0:T(1,128)S(1)}, s32[1,32]{1,0:T(1,128)}, u32[]{:S(2)}) copy-start(s32[1,32]{1,0:T(1,128)} %picks_ref.1) | copy-start | bytes 388
  4.0 1.3 %copy-start.1 = (bf16[1024,576]{1,0:T(8,128)(2,1)S(1)}, bf16[1024,576]{1,0:T(8,128)(2,1)}, u32[]{:S(2)}) copy-start(bf16[1024,576]{1,0:T(8,128)(2,1)} %copy.7) | copy-start | bytes 3538948
  71.0 4.3 %copy-start.3 = (s32[16]{0:T(128)S(1)}, s32[16]{0:T(128)}, u32[]{:S(2)}) copy-start(s32[16]{0:T(128)} %lengths_ref.1) | copy-start | bytes 196
  75.4 1.7 %copy-start = (bf16[16,128,576]{2,1,0:T(8,128)(2,1)S(1)}, bf16[16,128,576]{2,1,0:T(8,128)(2,1)}, u32[]{:S(2)}) copy-start(bf16[16,128,576]{2,1,0:T(8,128)(2,1)} %copy.8.q_ref) | copy-start | bytes 7077892

commit v2 on v1

v2 whole, which is shorter than its diff:
```python
import functools

import jax
import jax.numpy as jnp
from jax import lax
from jax.experimental import pallas as pl
from jax.experimental.pallas import tpu as pltpu
from jax.sharding import PartitionSpec as P

LAT = 512
BLOCK = 64
TOPK = 32
LANES = 128

SOFTMAX_SCALE = 192.0 ** (-0.5)
LOG2E = 1.4426950408889634
MESH = pl.DeviceIdType.MESH
HIDDEN = -1e30


def step_kernel(
    ctx_count, owned, units, picks_ref, lengths_ref, queries_ref, cache_ref, out_ref,
    raw_q, q_ref, flags_ref, all_flags, gath, pool, keys_t, values, positions, order,
    top_ref, total_ref, acc_ref, q_sem, flag_send, flag_recv, send, recv,
):
    rows, feature, heads = queries_ref.shape
    rope = feature - LAT
    pair = 2 * BLOCK
    tall = pair * rope // LAT
    line = ctx_count // 4
    late_blocks = 2 * units
    early_blocks = TOPK - late_blocks
    me = lax.axis_index("ctx")
    core = lax.rem(me, 2)
    y = lax.rem(me // 2, 2)
    z = me // 4
    far = jnp.where(2 * z < line, line - 1, 0)

    fetch = pltpu.make_async_copy(queries_ref, raw_q, q_sem)
    fetch.start()

    def at(zz, yy, cc):
        return (zz * 2 + yy) * 2 + cc

    barrier = pltpu.get_barrier_semaphore()

    @pl.loop(1, ctx_count)
    def _(d):
        pl.semaphore_signal(
            barrier, inc=1, device_id={"ctx": lax.rem(me + d, ctx_count)}, device_id_type=MESH
        )

    flag_rows = flags_ref.shape[0]
    block_id = lax.broadcasted_iota(jnp.int32, (flag_rows, LANES), 0) * LANES
    block_id += lax.broadcasted_iota(jnp.int32, (flag_rows, LANES), 1)
    lane = lax.broadcasted_iota(jnp.int32, (1, LANES), 1)
    flags = jnp.zeros((flag_rows, LANES), jnp.int32)
    ordered = jnp.zeros((1, LANES), jnp.int32)
    early_seen = jnp.int32(0)
    for k in range(TOPK):
        p = picks_ref[0, k]
        owner = p // owned
        is_late = (owner // 4 == far) & (lax.rem(owner // 2, 2) != y)
        place = jnp.where(is_late, TOPK - 1 - (k - early_seen), early_seen)
        early_seen += jnp.where(is_late, 0, 1)
        flags = jnp.where(block_id == p, 1, flags)
        ordered = jnp.where(lane == place, p, ordered)
    flags_ref[...] = flags

    pl.semaphore_wait(barrier, ctx_count - 1)

    def flag_copy(d):
        return pltpu.make_async_remote_copy(
            src_ref=flags_ref,
            dst_ref=all_flags.at[me],
            send_sem=flag_send.at[d],
            recv_sem=flag_recv.at[me],
            device_id={"ctx": lax.rem(me + d, ctx_count)},
            device_id_type=MESH,
        )

    def flag_arrival(source):
        return pltpu.make_async_remote_copy(
            src_ref=flags_ref,
            dst_ref=all_flags.at[source],
            send_sem=flag_send.at[0],
            recv_sem=flag_recv.at[source],
            device_id={"ctx": source},
            device_id_type=MESH,
        )

    @pl.loop(1, ctx_count)
    def _(d):
        flag_copy(d).start()

    all_flags[me] = flags

    @pl.loop(1, ctx_count)
    def _(d):
        flag_arrival(lax.rem(me + d, ctx_count)).wait_recv()

    named = jnp.minimum(jnp.max(all_flags[...], axis=0), 1)
    mine = (named > 0) & (block_id // owned == me)

    def unit_copy(slot, local, way, target):
        return pltpu.make_async_remote_copy(
            src_ref=gath.at[slot],
            dst_ref=gath.at[slot],
            send_sem=send.at[local, way],
            recv_sem=recv.at[slot],
            device_id={"ctx": target},
            device_id_type=MESH,
        )

    def slot_of(zz, j):
        crossed = (j == units).astype(jnp.int32)
        yy = lax.rem(y + crossed, 2)
        u = j * (1 - crossed)
        return at(zz, yy, core) * units + u, (zz * 2 + yy) * units + u

    up = at(lax.rem(z + 1, line), y, core)
    down = at(lax.rem(z + line - 1, line), y, core)
    across = at(z, 1 - y, core)
    sibling = at(z, y, 1 - core)

    def sends(zz, j):
        valid = (zz >= 0) & (zz < line) & ((j < units) | (core == 1))
        own_line = j < units
        return (
            (0, up, valid & (zz <= z) & (z + 1 < line)),
            (1, down, valid & (zz >= z) & (z > 0)),
            (2, across, valid & own_line & ((zz == z) | (core == 0) | (j > 0))),
            (3, sibling, valid),
        )

    def forward(zz, j, skip=()):
        slot, local = slot_of(zz, j)
        for way, target, yes in sends(zz, j):
            if way not in skip:
                @pl.when(yes)
                def _():
                    unit_copy(slot, local, way, target).start()

    def arrived(slot):
        unit_copy(slot, 0, 0, sibling).wait_recv()

    past = ctx_count * owned
    last = jnp.int32(-1)
    token = lax.broadcasted_iota(jnp.int32, (pair, owned * BLOCK), 0)
    column = lax.broadcasted_iota(jnp.int32, (pair, owned * BLOCK), 1)
    for u in range(units):
        starts = []
        for h in range(2):
            last = jnp.min(jnp.where(mine & (block_id > last), block_id, past))
            starts.append(jnp.minimum(last - me * owned, owned - 1) * BLOCK)
        wanted = jnp.where(token < BLOCK, starts[0] + token, starts[1] + token - BLOCK)
        chosen = jnp.where(column == wanted, 1.0, 0.0).astype(jnp.bfloat16)
        tokens = lax.dot_general(
            chosen, cache_ref[...], (((1,), (1,)), ((), ())), preferred_element_type=jnp.float32
        ).astype(jnp.bfloat16)
        tail = tokens[:, LAT:]
        packed = jnp.concatenate(
            [tail[i * tall : (i + 1) * tall, :] for i in range(pair // tall)], axis=1
        )
        gath[me * units + u, :pair, :] = tokens[:, :LAT]
        gath[me * units + u, pair:, :] = packed
        pool[me * units + u, :pair, :] = tokens[:, :LAT]
        pool[me * units + u, pair:, :] = packed
        forward(z, jnp.int32(u))

    def keep(slot):
        pool[slot] = gath[slot]

    fetch.wait()

    def turn(row):
        q_ref[row] = raw_q[row].T

    for k in range(TOPK):
        order[k] = jnp.sum(jnp.where(lane == k, ordered, 0))

    per = units + 1

    @pl.loop(0, per * (line - 1))
    def _(k):
        step = k // per
        j = lax.rem(k, per)
        for zz in (z + 1 + step, z - 1 - step):
            @pl.when((zz >= 0) & (zz < line) & ((j < units) | (core == 1)))
            def _():
                slot, _ = slot_of(zz, j)
                arrived(slot)
                forward(zz, j)
                keep(slot)

        @pl.when((k == 0) & (core == 1))
        def _():
            slot, _ = slot_of(z, jnp.int32(units))
            arrived(slot)
            forward(z, jnp.int32(units))
            keep(slot)

        @pl.when(k < rows)
        def _():
            turn(lax.rem(k, rows))

    @pl.loop(min(rows, per * (line - 1)), rows)
    def _(row):
        turn(row)

    def cross(zz, j):
        @pl.when((core == 0) | (j > 0))
        def _():
            slot = at(zz, 1 - y, core) * units + j
            local = (zz * 2 + 1 - y) * units + j
            arrived(slot)
            unit_copy(slot, local, 3, sibling).start()
            keep(slot)

    def beside(owner, u):
        slot = owner * units + u
        arrived(slot)
        keep(slot)

    @pl.loop(0, units * line)
    def _(k):
        zz = lax.rem(z + k // units, line)

        @pl.when(zz != far)
        def _():
            cross(zz, lax.rem(k, units))

    @pl.loop(0, line * 2 * units)
    def _(k):
        o = k // units

        @pl.when((o // 2 != far) | (lax.rem(o, 2) == y))
        def _():
            beside(o * 2 + 1 - core, lax.rem(k, units))

    def fill(first_block, blocks):
        for k in range(first_block, first_block + blocks, 2):
            latent, tails, places = [], [], []
            for h in range(2):
                p = order[k + h]
                owner = p // owned
                slot = jnp.sum(jnp.where((block_id // owned == owner) & (block_id < p), named, 0))
                unit = pool[owner * units + slot // 2]
                first = lax.rem(slot, 2) == 0
                latent.append(jnp.where(first, unit[:BLOCK], unit[BLOCK:pair]))
                tail = jnp.where(first, unit[pair:, : LAT // 2], unit[pair:, LAT // 2 :])
                tails += [tail[:, i * rope : (i + 1) * rope] for i in range(BLOCK // tall)]
                places.append(p * BLOCK)
            latent = jnp.concatenate(latent, axis=0)
            tails = jnp.concatenate(tails, axis=0)
            span = slice(k * BLOCK, (k + 2) * BLOCK)
            values[span, :] = latent
            keys_t[:LAT, span] = latent.T
            keys_t[LAT:, span] = tails.T
            positions[:, span] = jnp.where(lane < BLOCK, places[0] + lane, places[1] + lane - BLOCK)

    scale = SOFTMAX_SCALE * LOG2E
    pairs = rows // 2

    def scores(i, span):
        q = q_ref[pl.ds(2 * i, 2)].reshape(2 * heads, feature)
        s = jnp.dot(q, keys_t[:, span], preferred_element_type=jnp.float32)
        where = positions[:, span]
        return jnp.concatenate(
            [
                jnp.where(where < lengths_ref[2 * i + r], s[r * heads : (r + 1) * heads], HIDDEN)
                for r in range(2)
            ],
            axis=0,
        )

    early = slice(0, early_blocks * BLOCK)
    late = slice(early_blocks * BLOCK, TOPK * BLOCK)
    fill(0, early_blocks)

    @pl.loop(0, pairs)
    def _(i):
        s = scores(i, early)
        top = jnp.max(s, axis=1, keepdims=True)
        e = jnp.exp2((s - top) * scale)
        top_ref[i] = top
        total_ref[i] = jnp.sum(e, axis=1, keepdims=True)
        acc_ref[i] = jnp.dot(
            e.astype(jnp.bfloat16), values[early, :], preferred_element_type=jnp.float32
        )

        @pl.when(lax.rem(i, 2) == 1)
        def _():
            @pl.when(i // 2 < units)
            def _():
                cross(far, i // 2)

    @pl.loop(min(units, pairs // 2), units)
    def _(u):
        cross(far, u)

    @pl.loop(0, units)
    def _(u):
        beside(at(far, 1 - y, 1 - core), u)

    fill(early_blocks, late_blocks)

    @pl.loop(0, pairs)
    def _(i):
        s = scores(i, late)
        before = top_ref[i]
        top = jnp.maximum(before, jnp.max(s, axis=1, keepdims=True))
        e = jnp.exp2((s - top) * scale)
        shrink = jnp.exp2((before - top) * scale)
        total = total_ref[i] * shrink + jnp.sum(e, axis=1, keepdims=True)
        o = acc_ref[i] * shrink + jnp.dot(
            e.astype(jnp.bfloat16), values[late, :], preferred_element_type=jnp.float32
        )
        out_ref[pl.ds(2 * i, 2)] = (o / total).astype(jnp.bfloat16).reshape(2, heads, LAT)

    @pl.loop(1, ctx_count)
    def _(d):
        flag_copy(d).wait_send()

    @pl.loop(0, per * line)
    def _(k):
        zz = k // per
        j = lax.rem(k, per)
        slot, local = slot_of(zz, j)
        for way, target, yes in sends(zz, j):
            @pl.when(yes)
            def _():
                unit_copy(slot, local, way, target).wait_send()

    @pl.loop(0, units * line)
    def _(k):
        zz = k // units
        j = lax.rem(k, units)

        @pl.when((core == 0) | (j > 0))
        def _():
            slot = at(zz, 1 - y, core) * units + j
            local = (zz * 2 + 1 - y) * units + j
            unit_copy(slot, local, 3, sibling).wait_send()


def shards(queries, latent_cache, block_picks, lengths):
    ctx_count = lax.axis_size("ctx")
    rows, heads, feature = queries.shape
    owned = latent_cache.shape[0] // BLOCK
    units = max(1, 2 * TOPK // ctx_count)
    flag_rows = -(-(ctx_count * owned) // LANES // 8) * 8
    tall = 2 * BLOCK + 2 * BLOCK * (feature - LAT) // LAT
    keys = TOPK * BLOCK
    return pl.pallas_call(
        functools.partial(step_kernel, ctx_count, owned, units),
        out_shape=jax.ShapeDtypeStruct((rows, heads, LAT), jnp.bfloat16),
        in_specs=[
            pl.BlockSpec(memory_space=pltpu.SMEM),
            pl.BlockSpec(memory_space=pltpu.SMEM),
            pl.BlockSpec(memory_space=pl.ANY),
            pl.BlockSpec(memory_space=pltpu.VMEM),
        ],
        out_specs=pl.BlockSpec(memory_space=pltpu.VMEM),
        scratch_shapes=[
            pltpu.VMEM((rows, feature, heads), jnp.bfloat16),
            pltpu.VMEM((rows, heads, feature), jnp.bfloat16),
            pltpu.VMEM((flag_rows, LANES), jnp.int32),
            pltpu.VMEM((ctx_count, flag_rows, LANES), jnp.int32),
            pltpu.VMEM((ctx_count * units, tall, LAT), jnp.bfloat16),
            pltpu.VMEM((ctx_count * units, tall, LAT), jnp.bfloat16),
            pltpu.VMEM((feature, keys), jnp.bfloat16),
            pltpu.VMEM((keys, LAT), jnp.bfloat16),
            pltpu.VMEM((1, keys), jnp.int32),
            pltpu.SMEM((TOPK,), jnp.int32),
            pltpu.VMEM((rows // 2, 2 * heads, 1), jnp.float32),
            pltpu.VMEM((rows // 2, 2 * heads, 1), jnp.float32),
            pltpu.VMEM((rows // 2, 2 * heads, LAT), jnp.float32),
            pltpu.SemaphoreType.DMA,
            pltpu.SemaphoreType.DMA((ctx_count,)),
            pltpu.SemaphoreType.DMA((ctx_count,)),
            pltpu.SemaphoreType.DMA((ctx_count // 2 * units, 4)),
            pltpu.SemaphoreType.DMA((ctx_count * units,)),
        ],
        compiler_params=pltpu.CompilerParams(
            collective_id=0, has_side_effects=True, vmem_limit_bytes=60 * 1024 * 1024
        ),
    )(block_picks, lengths, jnp.swapaxes(queries, 1, 2), latent_cache.T)


def solution(mesh):
    placed = (
        P(("groups", "ctx"), None, None),
        P(("groups", "ctx"), None),
        P(("groups", "ctx"), None),
        P(("groups", "ctx")),
    )
    return jax.shard_map(
        shards,
        mesh=mesh,
        in_specs=placed,
        out_specs=P(("groups", "ctx"), None, None),
        check_vma=False,
    )
```

time: 94.4 us -> 87.9 us (0.931)
  local copies, waits for them, and re-layouts: 9.89 us -> 3.1 us
  other arithmetic: 1.54 us -> 0 us
  Pallas kernels: 82.6 us -> 83.9 us
    unnamed x10 -> x1, local copies, waits for them, and re-layouts: 9.8 us -> 3.1 us
    pallas_call x2 -> x1, Pallas kernels: 82.6 us -> 83.9 us  [shards(): pl.pallas_call(functools.partial(step_kernel, ctx_count, owned, units), o...]
where the time goes in v2:
time: 87.9 us; the launch traced here: 87 us
  Pallas kernels  83.9 us (95%)
  local copies, waits for them, and re-layouts  3.1 us (4%)
    pallas_call x1, Pallas kernels, shards(): pl.pallas_call(functools.partial(step_kernel, ctx_count, owned, units), o...  83.9 us
    unnamed x1, local copies, waits for them, and re-layouts  3.1 us

profile of v2, /device:TPU:0, one launch (start us, length us, event | category | flops | bytes accessed | tf_op | source)
XLA Modules:
  0.0 87.0 jit_solution(701300440458094832)
XLA Ops:
  0.0 83.9 %shard_map.46 = bf16[16,128,512]{2,1,0:T(8,128)(2,1)} custom-call(s32[1,32]{1,0:T(1,128)} %picks_ref.1, s32[16]{0:T(128)} %lengths_ref.1, bf16[16,576,128]{2,1,0:T(8,128)(2,1)} %bitcast.2, bf16[576,1024]{1,0:T(8,128)(2,1)} %bitcast.3), custom_call_target="tpu_custom_call" | custom-call | tf_op jit(solution)/shard_map/pallas_call | solution.py:355
  83.9 3.1 %copy.6 = bf16[16,128,512]{2,1,0:T(8,128)(2,1)} copy(bf16[16,128,512]{2,1,0:T(8,128)(2,1)} %shard_map.46) | data formatting | bytes 4194304

commit v3 on v2

--- a/solution.py
+++ b/solution.py
@@ -20,15 +20,15 @@
 
 def step_kernel(
     ctx_count, owned, units, picks_ref, lengths_ref, queries_ref, cache_ref, out_ref,
-    raw_q, q_ref, flags_ref, all_flags, gath, pool, keys_t, values, positions, order,
-    top_ref, total_ref, acc_ref, q_sem, flag_send, flag_recv, send, recv,
+    raw_q, near_cache, q_ref, flags_ref, all_flags, gath, pool, keys_t, values, positions, order,
+    top_ref, total_ref, acc_ref, q_sem, cache_sem, flag_send, flag_recv, send, recv,
 ):
     rows, feature, heads = queries_ref.shape
     rope = feature - LAT
     pair = 2 * BLOCK
     tall = pair * rope // LAT
     line = ctx_count // 4
-    late_blocks = 2 * units
+    late_blocks = 4 * units
     early_blocks = TOPK - late_blocks
     me = lax.axis_index("ctx")
     core = lax.rem(me, 2)
@@ -37,6 +37,8 @@
     far = jnp.where(2 * z < line, line - 1, 0)
 
     fetch = pltpu.make_async_copy(queries_ref, raw_q, q_sem)
+    fetch_cache = pltpu.make_async_copy(cache_ref, near_cache, cache_sem)
+    fetch_cache.start()
     fetch.start()
 
     def at(zz, yy, cc):
@@ -60,7 +62,7 @@
     for k in range(TOPK):
         p = picks_ref[0, k]
         owner = p // owned
-        is_late = (owner // 4 == far) & (lax.rem(owner // 2, 2) != y)
+        is_late = owner // 4 == far
         place = jnp.where(is_late, TOPK - 1 - (k - early_seen), early_seen)
         early_seen += jnp.where(is_late, 0, 1)
         flags = jnp.where(block_id == p, 1, flags)
@@ -145,6 +147,7 @@
         unit_copy(slot, 0, 0, sibling).wait_recv()
 
     past = ctx_count * owned
+    fetch_cache.wait()
     last = jnp.int32(-1)
     token = lax.broadcasted_iota(jnp.int32, (pair, owned * BLOCK), 0)
     column = lax.broadcasted_iota(jnp.int32, (pair, owned * BLOCK), 1)
@@ -156,7 +159,7 @@
         wanted = jnp.where(token < BLOCK, starts[0] + token, starts[1] + token - BLOCK)
         chosen = jnp.where(column == wanted, 1.0, 0.0).astype(jnp.bfloat16)
         tokens = lax.dot_general(
-            chosen, cache_ref[...], (((1,), (1,)), ((), ())), preferred_element_type=jnp.float32
+            chosen, near_cache[...], (((1,), (1,)), ((), ())), preferred_element_type=jnp.float32
         ).astype(jnp.bfloat16)
         tail = tokens[:, LAT:]
         packed = jnp.concatenate(
@@ -181,8 +184,7 @@
 
     per = units + 1
 
-    @pl.loop(0, per * (line - 1))
-    def _(k):
+    def along(k):
         step = k // per
         j = lax.rem(k, per)
         for zz in (z + 1 + step, z - 1 - step):
@@ -193,6 +195,12 @@
                 forward(zz, j)
                 keep(slot)
 
+    main = per * (line - 2)
+
+    @pl.loop(0, main)
+    def _(k):
+        along(k)
+
         @pl.when((k == 0) & (core == 1))
         def _():
             slot, _ = slot_of(z, jnp.int32(units))
@@ -204,7 +212,7 @@
         def _():
             turn(lax.rem(k, rows))
 
-    @pl.loop(min(rows, per * (line - 1)), rows)
+    @pl.loop(min(rows, main), rows)
     def _(row):
         turn(row)
 
@@ -226,6 +234,10 @@
     def _(k):
         zz = lax.rem(z + k // units, line)
 
+        @pl.when(k // units == line - 2)
+        def _():
+            along(main + lax.rem(k, units))
+
         @pl.when(zz != far)
         def _():
             cross(zz, lax.rem(k, units))
@@ -234,7 +246,7 @@
     def _(k):
         o = k // units
 
-        @pl.when((o // 2 != far) | (lax.rem(o, 2) == y))
+        @pl.when(o // 2 != far)
         def _():
             beside(o * 2 + 1 - core, lax.rem(k, units))
 
@@ -260,7 +272,8 @@
             positions[:, span] = jnp.where(lane < BLOCK, places[0] + lane, places[1] + lane - BLOCK)
 
     scale = SOFTMAX_SCALE * LOG2E
-    pairs = rows // 2
+    merged = 2 if rows % 4 == 0 else 1
+    groups = rows // 2 // merged
 
     def scores(i, span):
         q = q_ref[pl.ds(2 * i, 2)].reshape(2 * heads, feature)
@@ -278,45 +291,49 @@
     late = slice(early_blocks * BLOCK, TOPK * BLOCK)
     fill(0, early_blocks)
 
-    @pl.loop(0, pairs)
-    def _(i):
-        s = scores(i, early)
-        top = jnp.max(s, axis=1, keepdims=True)
-        e = jnp.exp2((s - top) * scale)
-        top_ref[i] = top
-        total_ref[i] = jnp.sum(e, axis=1, keepdims=True)
-        acc_ref[i] = jnp.dot(
-            e.astype(jnp.bfloat16), values[early, :], preferred_element_type=jnp.float32
-        )
-
-        @pl.when(lax.rem(i, 2) == 1)
-        def _():
-            @pl.when(i // 2 < units)
-            def _():
-                cross(far, i // 2)
-
-    @pl.loop(min(units, pairs // 2), units)
+    @pl.loop(0, groups)
+    def _(g):
+        for m in range(merged):
+            i = g * merged + m
+            s = scores(i, early)
+            top = jnp.max(s, axis=1, keepdims=True)
+            e = jnp.exp2((s - top) * scale)
+            top_ref[i] = top
+            total_ref[i] = jnp.sum(e, axis=1, keepdims=True)
+            acc_ref[i] = jnp.dot(
+                e.astype(jnp.bfloat16), values[early, :], preferred_element_type=jnp.float32
+            )
+
+        @pl.when(g < units)
+        def _():
+            cross(far, g)
+
+    @pl.loop(min(units, groups), units)
     def _(u):
         cross(far, u)
 
-    @pl.loop(0, units)
-    def _(u):
-        beside(at(far, 1 - y, 1 - core), u)
+    along(jnp.int32(main + units))
+
+    @pl.loop(0, 2 * units)
+    def _(k):
+        beside(at(far, k // units, 1 - core), lax.rem(k, units))
 
     fill(early_blocks, late_blocks)
 
-    @pl.loop(0, pairs)
-    def _(i):
-        s = scores(i, late)
-        before = top_ref[i]
-        top = jnp.maximum(before, jnp.max(s, axis=1, keepdims=True))
-        e = jnp.exp2((s - top) * scale)
-        shrink = jnp.exp2((before - top) * scale)
-        total = total_ref[i] * shrink + jnp.sum(e, axis=1, keepdims=True)
-        o = acc_ref[i] * shrink + jnp.dot(
-            e.astype(jnp.bfloat16), values[late, :], preferred_element_type=jnp.float32
-        )
-        out_ref[pl.ds(2 * i, 2)] = (o / total).astype(jnp.bfloat16).reshape(2, heads, LAT)
+    @pl.loop(0, groups)
+    def _(g):
+        for m in range(merged):
+            i = g * merged + m
+            s = scores(i, late)
+            before = top_ref[i]
+            top = jnp.maximum(before, jnp.max(s, axis=1, keepdims=True))
+            e = jnp.exp2((s - top) * scale)
+            shrink = jnp.exp2((before - top) * scale)
+            total = total_ref[i] * shrink + jnp.sum(e, axis=1, keepdims=True)
+            o = acc_ref[i] * shrink + jnp.dot(
+                e.astype(jnp.bfloat16), values[late, :], preferred_element_type=jnp.float32
+            )
+            out_ref[pl.ds(2 * i, 2)] = (o / total).astype(jnp.bfloat16).reshape(2, heads, LAT)
 
     @pl.loop(1, ctx_count)
     def _(d):
@@ -359,11 +376,12 @@
             pl.BlockSpec(memory_space=pltpu.SMEM),
             pl.BlockSpec(memory_space=pltpu.SMEM),
             pl.BlockSpec(memory_space=pl.ANY),
-            pl.BlockSpec(memory_space=pltpu.VMEM),
+            pl.BlockSpec(memory_space=pl.ANY),
         ],
         out_specs=pl.BlockSpec(memory_space=pltpu.VMEM),
         scratch_shapes=[
             pltpu.VMEM((rows, feature, heads), jnp.bfloat16),
+            pltpu.VMEM((feature, owned * BLOCK), jnp.bfloat16),
             pltpu.VMEM((rows, heads, feature), jnp.bfloat16),
             pltpu.VMEM((flag_rows, LANES), jnp.int32),
             pltpu.VMEM((ctx_count, flag_rows, LANES), jnp.int32),
@@ -376,6 +394,7 @@
             pltpu.VMEM((rows // 2, 2 * heads, 1), jnp.float32),
             pltpu.VMEM((rows // 2, 2 * heads, 1), jnp.float32),
             pltpu.VMEM((rows // 2, 2 * heads, LAT), jnp.float32),
+            pltpu.SemaphoreType.DMA,
             pltpu.SemaphoreType.DMA,
             pltpu.SemaphoreType.DMA((ctx_count,)),
             pltpu.SemaphoreType.DMA((ctx_count,)),

time: 87.9 us -> 82 us (0.933)
  Pallas kernels: 83.9 us -> 78.7 us
    pallas_call x1, Pallas kernels: 83.9 us -> 78.7 us  [shards(): pl.pallas_call(functools.partial(step_kernel, ctx_count, owned, units), o...]
where the time goes in v3:
time: 82 us; the launch traced here: 81.8 us
  Pallas kernels  78.7 us (96%)
  local copies, waits for them, and re-layouts  3.1 us (4%)
    pallas_call x1, Pallas kernels, shards(): pl.pallas_call(functools.partial(step_kernel, ctx_count, owned, units), o...  78.7 us
    unnamed x1, local copies, waits for them, and re-layouts  3.1 us

profile of v3, /device:TPU:0, one launch (start us, length us, event | category | flops | bytes accessed | tf_op | source)
XLA Modules:
  0.0 81.8 jit_solution(2605058320554150366)
XLA Ops:
  0.0 78.7 %shard_map.46 = bf16[16,128,512]{2,1,0:T(8,128)(2,1)} custom-call(s32[1,32]{1,0:T(1,128)} %picks_ref.1, s32[16]{0:T(128)} %lengths_ref.1, bf16[16,576,128]{2,1,0:T(8,128)(2,1)} %bitcast.2, bf16[576,1024]{1,0:T(8,128)(2,1)} %bitcast.3), custom_call_target="tpu_custom_call" | custom-call | tf_op jit(solution)/shard_map/pallas_call | solution.py:372
  78.7 3.1 %copy.6 = bf16[16,128,512]{2,1,0:T(8,128)(2,1)} copy(bf16[16,128,512]{2,1,0:T(8,128)(2,1)} %shard_map.46) | data formatting | bytes 4194304
